TPU v7x, 32 devices: a whole 2x2x4 slice. The times are simulated.
32 devices in a mesh: grid: 4 (over y, x), fsdp: 8 (over z, core).
Axes of the slice: x: 2, y: 2, z: 4, core: 2. Of those that a mesh axis runs over, the one named last changes fastest.
Arguments:
- hidden: bfloat16 [512, 4096], P('fsdp'), may hold values from -16 to 16
- norm_gain: float32 [4096], replicated, may hold values from 0.5 to 1.5
- base_head: bfloat16 [8192, 4096], P('fsdp'), may hold values from -1 to 1
- first_dir: bfloat16 [8192, 4096], P('fsdp'), may hold values from -0.09375 to 0.09375
- second_dir: bfloat16 [8192, 4096], P('fsdp'), may hold values from -0.09375 to 0.09375
- coords: int32 [8, 2], P('grid'), parts along dimension 0, may hold values from 0 to 7
- targets: int32 [512], replicated, may hold values from 0 to 8191
Outputs:
- token_loss: float32 [8, 512], P('grid', 'fsdp'), parts along dimension 0
- mean_loss: float32 [8], P('grid'), parts along dimension 0
There are 4 independent parts, one for each index of `grid`. A program takes and returns all parts, laid end to end along the dimension named above; an argument that names none is the same for every part. Nothing has to cross between parts.
All inputs are finite; a program needn't handle non-finite values.
Results may differ from a plain program's by a relative error of at most 0.0003.
Values may be sent and summed in bfloat16 or wider, within the bound.
No kernel may reach another device: no remote copies, remote signals or barrier semaphores. Data moves between devices by JAX's collectives and lax.ppermute only.
A program may use at most 128 MiB of HBM per device.

v0:
```python
import functools
import jax
import jax.numpy as jnp
from jax import lax
from jax.experimental import pallas as pl
from jax.experimental.pallas import tpu as pltpu
from jax.sharding import PartitionSpec as P

epsilon = 1e-05


def mixing_of(coords):
    levels = jnp.arange(8, dtype=jnp.int32)
    level_table = (2.0 * levels.astype(jnp.float32) - 7.0) / 7.0
    chosen = (coords[:, :, None] == levels[None, None, :]).astype(jnp.float32)
    return jnp.sum(chosen * level_table, axis=2)


def swap(a, axis, mask):
    return lax.ppermute(a, axis, [(i, i ^ mask) for i in range(lax.axis_size(axis))])


def head_kernel(n_fsdp, n_grid, pts, shard_ref, *refs):
    mixing_refs, refs = refs[:n_grid], refs[n_grid:]
    chunks = refs[:n_fsdp]
    gain_ref, target_ref, base_ref, first_ref, second_ref, out_ref, rows_ref, dots_ref = refs[n_fsdp:]
    shard_idx = shard_ref[0]
    for j in range(n_fsdp):
        widened = chunks[j][...].astype(jnp.float32)
        inv_rms = lax.rsqrt(jnp.mean(widened * widened, axis=1, keepdims=True) + epsilon)
        rows_ref[shard_idx ^ j] = (widened * inv_rms * gain_ref[...]).astype(jnp.bfloat16)
    tokens = n_fsdp * chunks[0].shape[0]
    rows = rows_ref[...].reshape(tokens, rows_ref.shape[2])
    vocab_count = base_ref.shape[0]
    for k, weight_ref in enumerate((base_ref, first_ref, second_ref)):
        dots_ref[k] = lax.dot_general(
            rows, weight_ref[...], (((1,), (1,)), ((), ())), preferred_element_type=jnp.float32
        )
    columns = lax.broadcasted_iota(jnp.int32, (tokens, vocab_count), 1) + shard_idx * vocab_count
    matches = columns == target_ref[...]
    found = [
        jnp.sum(jnp.where(matches, dots_ref[k], 0.0), axis=1, keepdims=True) for k in range(3)
    ]
    lane = lax.broadcasted_iota(jnp.int32, (tokens, 128), 1)
    table = jnp.zeros((tokens, 128), jnp.float32)
    for p in range(n_grid * pts):
        mixing_ref, point = mixing_refs[p // pts], p % pts
        a, b = mixing_ref[point, 0], mixing_ref[point, 1]
        logits = dots_ref[0] + a * dots_ref[1] + b * dots_ref[2]
        top = jnp.max(logits, axis=1, keepdims=True)
        total = jnp.sum(jnp.exp(logits - top), axis=1, keepdims=True)
        row = (shard_ref[1] ^ (p // pts)) * 2 * pts + point
        table = jnp.where(lane == row, top + jnp.log(total), table)
        table = jnp.where(lane == row + pts, found[0] + a * found[1] + b * found[2], table)
    flipped = table.T
    for g in range(n_grid):
        block = flipped[g * 2 * pts : (g + 1) * 2 * pts]
        for f in range(n_fsdp):
            out_ref[g, f] = block


def load_kernel(shard_ref, rows_ref, mixing_ref, target_ref, *refs):
    count = (len(refs) - 1) // 2
    copies = [
        pltpu.make_async_copy(refs[k], refs[count + k], refs[-1].at[k]) for k in range(count)
    ]
    for copy in copies:
        copy.start()
    for copy in copies:
        copy.wait()


def loss_kernel(sub, shard_ref, got_ref, token_ref, mean_ref):
    n_grid, n_fsdp, _, tokens = got_ref.shape
    pts = token_ref.shape[0]
    shift = (n_fsdp - shard_ref[0]) * sub
    sums = jnp.zeros((pts, tokens), jnp.float32)
    for g in range(n_grid):
        parts = [got_ref[g, f] for f in range(n_fsdp)]
        top = functools.reduce(jnp.maximum, parts)
        total = sum(jnp.exp(part - top) for part in parts)
        lse = (top + jnp.log(total))[:pts]
        loss = lse - sum(parts)[pts:]
        sums = sums + loss
        token_ref[:, g * sub : (g + 1) * sub] = pltpu.roll(loss, shift, 1)[:, :sub]
    mean_ref[...] = jnp.sum(sums, axis=1, keepdims=True) / (n_grid * tokens)


def body(hidden, norm_gain, base_head, first_dir, second_dir, coords, targets):
    n_grid, n_fsdp = lax.axis_size("grid"), lax.axis_size("fsdp")
    grid_idx, shard_idx = lax.axis_index("grid"), lax.axis_index("fsdp")
    own_count, width = hidden.shape
    sub = own_count // n_grid
    tokens = n_fsdp * sub
    pts = coords.shape[0]
    vocab_count = base_head.shape[0]
    own = lax.dynamic_slice_in_dim(hidden, grid_idx * sub, sub, 0)
    slots = [None] * n_fsdp
    slots[0] = own
    for j in range(2, n_fsdp, 2):
        slots[j] = swap(own, "fsdp", j)
    for j in range(0, n_fsdp, 2):
        slots[j + 1] = swap(slots[j], "fsdp", 1)
    mine = mixing_of(coords)
    mixing = [mine]
    for j in range(1, n_grid):
        mixing.append(swap(mine, "grid", j))
    group_targets = lax.dynamic_index_in_dim(targets.reshape(n_fsdp, n_grid, sub), grid_idx, 1, False)
    group_targets = group_targets.reshape(tokens, 1)
    shard = jnp.stack([shard_idx, grid_idx]).astype(jnp.int32)

    smem = pl.BlockSpec(memory_space=pltpu.SMEM)
    vmem = pl.BlockSpec(memory_space=pltpu.VMEM)
    heads = [
        pltpu.with_memory_space_constraint(w, pltpu.HBM) for w in (base_head, first_dir, second_dir)
    ]
    anywhere = pl.BlockSpec(memory_space=pltpu.HBM)
    weights = pl.pallas_call(
        load_kernel,
        out_shape=tuple(pltpu.VMEM(w.shape, w.dtype) for w in heads),
        in_specs=[pl.BlockSpec(memory_space=pl.ANY)] * 4 + [anywhere] * 3,
        out_specs=(vmem,) * 3,
        scratch_shapes=[pltpu.SemaphoreType.DMA((3,))],
        compiler_params=pltpu.CompilerParams(vmem_limit_bytes=1024 * 1024),
        cost_estimate=pl.CostEstimate(flops=LOAD_FLOPS, transcendentals=0, bytes_accessed=6 * base_head.size),
        name="load_heads",
    )(shard, own, mine, group_targets, *heads)
    sent = pl.pallas_call(
        functools.partial(head_kernel, n_fsdp, n_grid, pts),
        out_shape=jax.ShapeDtypeStruct((n_grid, n_fsdp, 2 * pts, tokens), jnp.float32),
        in_specs=[smem] * (1 + n_grid) + [vmem] * (n_fsdp + 5),
        out_specs=vmem,
        scratch_shapes=[
            pltpu.VMEM((n_fsdp, sub, width), jnp.bfloat16),
            pltpu.VMEM((3, tokens, vocab_count), jnp.float32),
        ],
        compiler_params=pltpu.CompilerParams(vmem_limit_bytes=VMEM_LIMIT),
        name="head_stats",
    )(shard, *mixing, *slots, norm_gain.reshape(1, width), group_targets, *weights)
    got = lax.all_to_all(
        sent.reshape(n_grid * n_fsdp, 2 * pts, tokens), ("grid", "fsdp"), 0, 0
    ).reshape(n_grid, n_fsdp, 2 * pts, tokens)
    token_loss, mean_loss = pl.pallas_call(
        functools.partial(loss_kernel, sub),
        out_shape=(
            jax.ShapeDtypeStruct((pts, own_count), jnp.float32),
            jax.ShapeDtypeStruct((pts, 1), jnp.float32),
        ),
        in_specs=[smem, vmem],
        out_specs=(vmem, vmem),
        compiler_params=pltpu.CompilerParams(vmem_limit_bytes=4 * 1024 * 1024),
        name="loss_join",
    )(shard, got)
    return (token_loss, mean_loss.reshape(pts))


LOAD_FLOPS = 40_000_000
VMEM_LIMIT = 16 * 1024 * 1024


def solution(mesh):
    placed = (
        P("fsdp", None),
        P(),
        P("fsdp", None),
        P("fsdp", None),
        P("fsdp", None),
        P("grid", None),
        P(),
    )
    return jax.shard_map(
        body, mesh=mesh, in_specs=placed, out_specs=(P("grid", "fsdp"), P("grid")), check_vma=False
    )
```

profile of v0, /device:TPU:0, one launch (start us, length us, event | category | flops | bytes accessed | tf_op | source)
XLA Modules:
  0.0 60.6 jit_solution(3718366250776891292)
XLA Ops:
  0.6 0.0 copy-start
  0.6 1.0 %copy-done = bf16[64,4096]{1,0:T(8,128)(2,1)S(1)} copy-done((bf16[64,4096]{1,0:T(8,128)(2,1)S(1)}, bf16[64,4096]{1,0:T(8,128)(2,1)}, u32[]{:S(2)}) %copy-start) | copy-done | bytes 524312
  1.7 5.1 %collective-permute-start.8 = (bf16[16,4096]{1,0:T(8,128)(2,1)S(1)}, bf16[16,4096]{1,0:T(8,128)(2,1)S(1)}, u32[]{:S(2)}, u32[]{:S(2)}) collective-permute-start(bf16[16,4096]{1,0:T(8,128)(2,1)S(1)} %constant_dynamic-slice_fusion.rows_ref.refs_4_), channel_id=1, source_target_pairs={{0,6},{1,7},{2,4},{3,5},{4,2},{5,3},{6,0},{7,1},{8,14},{9,15},{10,... | collective-permute-start | bytes 393224 | tf_op jit(solution)/shard_map/ppermute | solution.py:20
  6.8 0.0 collective-permute-start.6
  6.8 0.6 %collective-permute-start.4 = (bf16[16,4096]{1,0:T(8,128)(2,1)S(1)}, bf16[16,4096]{1,0:T(8,128)(2,1)S(1)}, u32[]{:S(2)}, u32[]{:S(2)}) collective-permute-start(bf16[16,4096]{1,0:T(8,128)(2,1)S(1)} %constant_dynamic-slice_fusion.rows_ref.refs_4_), channel_id=1, source_target_pairs={{0,2},{1,3},{2,0},{3,1},{4,6},{5,7},{6,4},{7,5},{8,10},{9,11},{10,... | collective-permute-start | bytes 393224 | tf_op jit(solution)/shard_map/ppermute | solution.py:20
  7.5 0.0 collective-permute-start.3
  7.5 3.8 %collective-permute-done.8.refs_10_ = bf16[16,4096]{1,0:T(8,128)(2,1)S(1)} collective-permute-done((bf16[16,4096]{1,0:T(8,128)(2,1)S(1)}, bf16[16,4096]{1,0:T(8,128)(2,1)S(1)}, u32[]{:S(2)}, u32[]{:S(2)}) %collective-permute-start.8) | collective-permute-done | bytes 131104 | tf_op jit(solution)/shard_map/ppermute | solution.py:20
  11.3 0.0 collective-permute-start.9
  11.3 6.6 %collective-permute-done.6.refs_8_ = bf16[16,4096]{1,0:T(8,128)(2,1)S(1)} collective-permute-done((bf16[16,4096]{1,0:T(8,128)(2,1)S(1)}, bf16[16,4096]{1,0:T(8,128)(2,1)S(1)}, u32[]{:S(2)}, u32[]{:S(2)}) %collective-permute-start.6) | collective-permute-done | bytes 131104 | tf_op jit(solution)/shard_map/ppermute | solution.py:20
  17.9 0.0 collective-permute-start.7
  17.9 0.0 collective-permute-done.4.refs_6_
  17.9 0.5 collective-permute-start.5
  18.4 0.8 %fusion.mixing_ref.refs_0_ = f32[2,2]{1,0:T(2,128)S(1)} fusion(f32[8]{0:T(128)S(1)} %add_multiply_fusion, s32[2,2]{1,0:T(2,128)} %param.12), kind=kLoop, calls=%fused_computation.2 | loop fusion | flops 92 | bytes 64 | tf_op jit(solution)/shard_map/reduce_sum | solution.py:16
  19.3 2.4 %collective-permute-start.2 = (f32[2,2]{1,0:T(2,128)S(1)}, f32[2,2]{1,0:T(2,128)S(1)}, u32[]{:S(2)}, u32[]{:S(2)}) collective-permute-start(f32[2,2]{1,0:T(2,128)S(1)} %fusion.mixing_ref.refs_0_), channel_id=1, source_target_pairs={{0,24},{8,16},{16,8},{24,0},{1,25},{9,17},{17,9},{25,1},{2,26},{10... | collective-permute-start | bytes 56 | tf_op jit(solution)/shard_map/ppermute | solution.py:20
  21.7 0.8 %reshape.32 = s32[8,4,16]{2,1,0:T(4,128)S(1)} reshape(s32[512]{0:T(512)} %param.13) | data formatting | bytes 4096 | tf_op jit(solution)/shard_map/reshape | solution.py:108
  22.5 0.1 reshape.37.target_ref.refs_13_
  22.6 0.1 pad_add_fusion.shard_ref
  22.7 8.2 %load_heads.1 = (bf16[1024,4096]{1,0:T(8,128)(2,1)S(1)}, bf16[1024,4096]{1,0:T(8,128)(2,1)S(1)}, bf16[1024,4096]{1,0:T(8,128)(2,1)S(1)}) custom-call(s32[2]{0:T(128)S(1)} %pad_add_fusion.shard_ref, bf16[16,4096]{1,0:T(8,128)(2,1)S(1)} %constant_dynamic-slice_fusion.rows_ref.refs_4_, f32[2,2]{1,0:T(2,128)S(1)} %fusion.mixing_ref.refs_0_, ...), custom_call_target="tpu_custom_call" | custom-call | flops 40000000 | bytes 25165824 | tf_op jit(solution)/shard_map/load_heads/pallas_call | solution.py:118
  30.9 0.0 collective-permute-done.2.refs_3_
  30.9 0.6 collective-permute-start.1
  31.4 3.1 %collective-permute-done.1.refs_2_ = f32[2,2]{1,0:T(2,128)S(1)} collective-permute-done((f32[2,2]{1,0:T(2,128)S(1)}, f32[2,2]{1,0:T(2,128)S(1)}, u32[]{:S(2)}, u32[]{:S(2)}) %collective-permute-start.1) | collective-permute-done | bytes 48 | tf_op jit(solution)/shard_map/ppermute | solution.py:20
  34.5 0.5 collective-permute-start
  35.1 3.0 %collective-permute-done.refs_1_ = f32[2,2]{1,0:T(2,128)S(1)} collective-permute-done((f32[2,2]{1,0:T(2,128)S(1)}, f32[2,2]{1,0:T(2,128)S(1)}, u32[]{:S(2)}, u32[]{:S(2)}) %collective-permute-start) | collective-permute-done | bytes 48 | tf_op jit(solution)/shard_map/ppermute | solution.py:20
  38.1 0.0 collective-permute-done.3.refs_5_
  38.1 0.0 collective-permute-done.9.refs_11_
  38.1 0.0 collective-permute-done.7.refs_9_
  38.1 0.0 collective-permute-done.5.refs_7_
  38.1 0.0 copy-done.1
  38.1 10.5 %head_stats.1 = f32[4,8,4,128]{3,2,1,0:T(4,128)S(1)} custom-call(s32[2]{0:T(128)S(1)} %pad_add_fusion.shard_ref, f32[2,2]{1,0:T(2,128)S(1)} %fusion.mixing_ref.refs_0_, f32[2,2]{1,0:T(2,128)S(1)} %collective-permute-done.refs_1_, f32[2,2]{1,0:T(2,128)S(1)} %collective-permute-done.1.refs_2_, f32[2,2]{1,0:T(2,128)S(1)} %collective-permute-done.2.refs_3_, ...), custom_call_target="tpu_custom_call" | custom-call | tf_op jit(solution)/shard_map/head_stats/pallas_call | solution.py:128
  48.6 10.0 %all_to_all.5 = f32[32,4,128]{2,1,0:T(4,128)S(1)} all-to-all(f32[32,4,128]{2,1,0:T(4,128)S(1)} %bitcast.5), channel_id=1, replica_groups=mesh['grid'=4,'fsdp'=8] {'grid','fsdp'}, dimensions={0} | all-to-all | bytes 131072 | tf_op jit(solution)/shard_map/all_to_all | solution.py:140
  58.7 1.3 %loss_join.1 = (f32[2,64]{1,0:T(2,128)}, f32[2,1]{1,0:T(2,128)S(1)}) custom-call(s32[2]{0:T(128)S(1)} %pad_add_fusion.shard_ref, f32[4,8,4,128]{3,2,1,0:T(4,128)S(1)} %bitcast.6), custom_call_target="tpu_custom_call" | custom-call | tf_op jit(solution)/shard_map/loss_join/pallas_call | solution.py:143
  60.0 0.6 %reduce.1 = f32[2]{0:T(128)} reduce(f32[2,1]{1,0:T(2,128)S(1)} %get-tuple-element.11, f32[]{:T(128)} %constant.31), dimensions={1}, to_apply=%get-tuple-element.11.reduce_sub_computation | reduce | bytes 20 | tf_op jit(solution)/shard_map/loss_join/pallas_call | solution.py:143
  (4 shorter events, 0.0 us)
Async XLA Ops:
  0.6 1.0 %copy-start = (bf16[64,4096]{1,0:T(8,128)(2,1)S(1)}, bf16[64,4096]{1,0:T(8,128)(2,1)}, u32[]{:S(2)}) copy-start(bf16[64,4096]{1,0:T(8,128)(2,1)} %param.7) | copy-start | bytes 1572868
  1.7 9.6 %collective-permute-start.8 = (bf16[16,4096]{1,0:T(8,128)(2,1)S(1)}, bf16[16,4096]{1,0:T(8,128)(2,1)S(1)}, u32[]{:S(2)}, u32[]{:S(2)}) collective-permute-start(bf16[16,4096]{1,0:T(8,128)(2,1)S(1)} %constant_dynamic-slice_fusion.rows_ref.refs_4_), channel_id=1, source_target_pairs={{0,6},{1,7},{2,4},{3,5},{4,2},{5,3},{6,0},{7,1},{8,14},{9,15},{10,... | collective-permute-start | bytes 393224 | tf_op jit(solution)/shard_map/ppermute | solution.py:20
  6.8 11.1 %collective-permute-start.6 = (bf16[16,4096]{1,0:T(8,128)(2,1)S(1)}, bf16[16,4096]{1,0:T(8,128)(2,1)S(1)}, u32[]{:S(2)}, u32[]{:S(2)}) collective-permute-start(bf16[16,4096]{1,0:T(8,128)(2,1)S(1)} %constant_dynamic-slice_fusion.rows_ref.refs_4_), channel_id=1, source_target_pairs={{0,4},{1,5},{2,6},{3,7},{4,0},{5,1},{6,2},{7,3},{8,12},{9,13},{10,... | collective-permute-start | bytes 393224 | tf_op jit(solution)/shard_map/ppermute | solution.py:20
  6.8 11.1 %collective-permute-start.4 = (bf16[16,4096]{1,0:T(8,128)(2,1)S(1)}, bf16[16,4096]{1,0:T(8,128)(2,1)S(1)}, u32[]{:S(2)}, u32[]{:S(2)}) collective-permute-start(bf16[16,4096]{1,0:T(8,128)(2,1)S(1)} %constant_dynamic-slice_fusion.rows_ref.refs_4_), channel_id=1, source_target_pairs={{0,2},{1,3},{2,0},{3,1},{4,6},{5,7},{6,4},{7,5},{8,10},{9,11},{10,... | collective-permute-start | bytes 393224 | tf_op jit(solution)/shard_map/ppermute | solution.py:20
  7.5 30.6 %collective-permute-start.3 = (bf16[16,4096]{1,0:T(8,128)(2,1)S(1)}, bf16[16,4096]{1,0:T(8,128)(2,1)S(1)}, u32[]{:S(2)}, u32[]{:S(2)}) collective-permute-start(bf16[16,4096]{1,0:T(8,128)(2,1)S(1)} %constant_dynamic-slice_fusion.rows_ref.refs_4_), channel_id=1, source_target_pairs={{0,1},{1,0},{2,3},{3,2},{4,5},{5,4},{6,7},{7,6},{8,9},{9,8},{10,11... | collective-permute-start | bytes 393224 | tf_op jit(solution)/shard_map/ppermute | solution.py:20
  11.3 26.8 %collective-permute-start.9 = (bf16[16,4096]{1,0:T(8,128)(2,1)S(1)}, bf16[16,4096]{1,0:T(8,128)(2,1)S(1)}, u32[]{:S(2)}, u32[]{:S(2)}) collective-permute-start(bf16[16,4096]{1,0:T(8,128)(2,1)S(1)} %collective-permute-done.8.refs_10_), channel_id=1, source_target_pairs={{0,1},{1,0},{2,3},{3,2},{4,5},{5,4},{6,7},{7,6},{8,9},{9,8},{10,11... | collective-permute-start | bytes 393224 | tf_op jit(solution)/shard_map/ppermute | solution.py:20
  17.9 20.2 %collective-permute-start.7 = (bf16[16,4096]{1,0:T(8,128)(2,1)S(1)}, bf16[16,4096]{1,0:T(8,128)(2,1)S(1)}, u32[]{:S(2)}, u32[]{:S(2)}) collective-permute-start(bf16[16,4096]{1,0:T(8,128)(2,1)S(1)} %collective-permute-done.6.refs_8_), channel_id=1, source_target_pairs={{0,1},{1,0},{2,3},{3,2},{4,5},{5,4},{6,7},{7,6},{8,9},{9,8},{10,11... | collective-permute-start | bytes 393224 | tf_op jit(solution)/shard_map/ppermute | solution.py:20
  17.9 20.2 %collective-permute-start.5 = (bf16[16,4096]{1,0:T(8,128)(2,1)S(1)}, bf16[16,4096]{1,0:T(8,128)(2,1)S(1)}, u32[]{:S(2)}, u32[]{:S(2)}) collective-permute-start(bf16[16,4096]{1,0:T(8,128)(2,1)S(1)} %collective-permute-done.4.refs_6_), channel_id=1, source_target_pairs={{0,1},{1,0},{2,3},{3,2},{4,5},{5,4},{6,7},{7,6},{8,9},{9,8},{10,11... | collective-permute-start | bytes 393224 | tf_op jit(solution)/shard_map/ppermute | solution.py:20
  19.3 11.6 %collective-permute-start.2 = (f32[2,2]{1,0:T(2,128)S(1)}, f32[2,2]{1,0:T(2,128)S(1)}, u32[]{:S(2)}, u32[]{:S(2)}) collective-permute-start(f32[2,2]{1,0:T(2,128)S(1)} %fusion.mixing_ref.refs_0_), channel_id=1, source_target_pairs={{0,24},{8,16},{16,8},{24,0},{1,25},{9,17},{17,9},{25,1},{2,26},{10... | collective-permute-start | bytes 56 | tf_op jit(solution)/shard_map/ppermute | solution.py:20
  22.7 15.4 %copy-start.1 = (f32[4096]{0:T(1024)S(1)}, f32[4096]{0:T(1024)}, u32[]{:S(2)}) copy-start(f32[4096]{0:T(1024)} %param.8) | copy-start | bytes 49156
  30.9 3.6 %collective-permute-start.1 = (f32[2,2]{1,0:T(2,128)S(1)}, f32[2,2]{1,0:T(2,128)S(1)}, u32[]{:S(2)}, u32[]{:S(2)}) collective-permute-start(f32[2,2]{1,0:T(2,128)S(1)} %fusion.mixing_ref.refs_0_), channel_id=1, source_target_pairs={{0,16},{8,24},{16,0},{24,8},{1,17},{9,25},{17,1},{25,9},{2,18},{10... | collective-permute-start | bytes 56 | tf_op jit(solution)/shard_map/ppermute | solution.py:20
  34.5 3.6 %collective-permute-start = (f32[2,2]{1,0:T(2,128)S(1)}, f32[2,2]{1,0:T(2,128)S(1)}, u32[]{:S(2)}, u32[]{:S(2)}) collective-permute-start(f32[2,2]{1,0:T(2,128)S(1)} %fusion.mixing_ref.refs_0_), channel_id=1, source_target_pairs={{0,8},{8,0},{16,24},{24,16},{1,9},{9,1},{17,25},{25,17},{2,10},{10... | collective-permute-start | bytes 56 | tf_op jit(solution)/shard_map/ppermute | solution.py:20
where the time goes:
time: 60.8 us; the launch traced here: 60.6 us
  Pallas kernels  20 us (33%)
  waiting for transfers between devices  16.5 us (27%)
  blocking collectives  10 us (16%)
  starting transfers between devices  9.85 us (16%)
  local copies, waits for them, and re-layouts  1.92 us (3%)
  other arithmetic  1.54 us (3%)
  between operations  0.72 us (1%)
    ppermute x10, waiting for transfers between devices, swap(): lax.ppermute(a, axis, [(i, i ^ mask) for i in range(lax.axis_size(axis))])  16.5 us
    pallas_call x1, Pallas kernels, body(): pl.pallas_call(functools.partial(head_kernel, n_fsdp, n_grid, pts), out_s...  10.5 us
    all_to_all x1, blocking collectives, body(): lax.all_to_all(sent.reshape(n_grid * n_fsdp, 2 * pts, tokens), ('grid', '...  10 us
    ppermute x10, starting transfers between devices, swap(): lax.ppermute(a, axis, [(i, i ^ mask) for i in range(lax.axis_size(axis))])  9.85 us
    pallas_call x1, Pallas kernels, body(): pl.pallas_call(load_kernel, out_shape=tuple((pltpu.VMEM(w.shape, w.dtype)...  8.19 us
    pallas_call x1, Pallas kernels, body(): pl.pallas_call(functools.partial(loss_kernel, sub), out_shape=(jax.ShapeD...  1.28 us
  transfers between devices with their start and end apart: 10, of which 4 were waited for; matrix products, arithmetic and copies ran while one was open for 3% of the time, Pallas kernels for 14%

commit v1 on v0

v1 whole, which is shorter than its diff:
```python
import functools
import math
import jax
import jax.numpy as jnp
from jax import lax
from jax.experimental import pallas as pl
from jax.experimental.pallas import tpu as pltpu
from jax.sharding import PartitionSpec as P

epsilon = 1e-05


def swap(a, axis, mask):
    return lax.ppermute(a, axis, [(i, i ^ mask) for i in range(lax.axis_size(axis))])


def head_kernel(n_fsdp, n_grid, pts, shard_ref, *refs):
    coords_refs, refs = refs[:n_grid], refs[n_grid:]
    chunks, refs = refs[:n_fsdp], refs[n_fsdp:]
    gain_ref, target_ref, base_ref, first_ref, second_hbm, out_ref = refs[:6]
    rows_ref, second_ref, dots_ref, arrived = refs[6:]
    fetch = pltpu.make_async_copy(second_hbm, second_ref, arrived)
    fetch.start()
    shard_idx, grid_idx = shard_ref[0], shard_ref[1]
    for j in range(n_fsdp):
        widened = chunks[j][...].astype(jnp.float32)
        inv_rms = lax.rsqrt(jnp.mean(widened * widened, axis=1, keepdims=True) + epsilon)
        rows_ref[shard_idx ^ j] = (widened * inv_rms * gain_ref[...]).astype(jnp.bfloat16)
    tokens = n_fsdp * chunks[0].shape[0]
    rows = rows_ref[...].reshape(tokens, rows_ref.shape[2])
    vocab_count = base_ref.shape[0]
    block = math.gcd(vocab_count, 256)

    def dot_of(weight):
        return lax.dot_general(
            weight, rows, (((1,), (1,)), ((), ())), preferred_element_type=jnp.float32
        )

    dots_ref[0] = dot_of(base_ref[...])
    dots_ref[1] = dot_of(first_ref[...])
    fetch.wait()
    points = []
    for j in range(n_grid):
        for p in range(pts):
            level = [jnp.full((8, tokens), coords_refs[j][p, k], jnp.int32) for k in range(2)]
            points.append([(2.0 * c.astype(jnp.float32) - 7.0) / 7.0 for c in level])
    state = [None] * len(points)
    found = [jnp.zeros((8, tokens), jnp.float32)] * 3
    row_of = 8 * lax.broadcasted_iota(jnp.int32, (block // 8, 8, tokens), 0)
    row_of = row_of + lax.broadcasted_iota(jnp.int32, (block // 8, 8, tokens), 1)
    wanted = target_ref[...] - shard_idx * vocab_count
    for start in range(0, vocab_count, block):
        span = pl.ds(start, block)
        parts = [dots_ref[0, span], dots_ref[1, span], dot_of(second_ref[span])]
        parts = [part.reshape(block // 8, 8, tokens) for part in parts]
        matches = row_of == (wanted - start)[None]
        found = [
            old + jnp.sum(jnp.where(matches, part, 0.0), axis=0) for old, part in zip(found, parts)
        ]
        for n, (a, b) in enumerate(points):
            logits = parts[0] + a[None] * parts[1] + b[None] * parts[2]
            top = jnp.max(logits, axis=0)
            if state[n] is not None:
                top = jnp.maximum(top, state[n][0])
            total = jnp.sum(jnp.exp(logits - top[None]), axis=0)
            if state[n] is not None:
                total = total + state[n][1] * jnp.exp(state[n][0] - top)
            state[n] = (top, total)
    for j in range(n_grid):
        lines = [[], []]
        for p in range(pts):
            (a, b), (tops, totals) = points[j * pts + p], state[j * pts + p]
            top = jnp.max(tops, axis=0, keepdims=True)
            total = jnp.sum(totals * jnp.exp(tops - top), axis=0, keepdims=True)
            lines[0].append(top + jnp.log(total))
            picked = found[0] + a * found[1] + b * found[2]
            lines[1].append(jnp.sum(picked, axis=0, keepdims=True))
        packed = jnp.concatenate(lines[0] + lines[1], axis=0)
        for f in range(n_fsdp):
            out_ref[grid_idx ^ j, f] = packed


def load_kernel(shard_ref, rows_ref, target_ref, *refs):
    count = (len(refs) - 1) // 2
    copies = [
        pltpu.make_async_copy(refs[k], refs[count + k], refs[-1].at[k]) for k in range(count)
    ]
    for copy in copies:
        copy.start()
    for copy in copies:
        copy.wait()


def loss_kernel(sub, shard_ref, got_ref, token_ref, mean_ref):
    n_grid, n_fsdp, _, tokens = got_ref.shape
    pts = token_ref.shape[0]
    shift = (n_fsdp - shard_ref[0]) * sub
    sums = jnp.zeros((pts, tokens), jnp.float32)
    for g in range(n_grid):
        parts = [got_ref[g, f] for f in range(n_fsdp)]
        top = functools.reduce(jnp.maximum, parts)
        total = sum(jnp.exp(part - top) for part in parts)
        lse = (top + jnp.log(total))[:pts]
        loss = lse - sum(parts)[pts:]
        sums = sums + loss
        token_ref[:, g * sub : (g + 1) * sub] = pltpu.roll(loss, shift, 1)[:, :sub]
    for p in range(pts):
        mean_ref[p] = jnp.sum(sums[p : p + 1]) / (n_grid * tokens)


def body(hidden, norm_gain, base_head, first_dir, second_dir, coords, targets):
    n_grid, n_fsdp = lax.axis_size("grid"), lax.axis_size("fsdp")
    grid_idx, shard_idx = lax.axis_index("grid"), lax.axis_index("fsdp")
    own_count, width = hidden.shape
    sub = own_count // n_grid
    tokens = n_fsdp * sub
    pts = coords.shape[0]
    vocab_count = base_head.shape[0]
    own = lax.dynamic_slice_in_dim(hidden, grid_idx * sub, sub, 0)
    slots = [None] * n_fsdp
    slots[0] = own
    for j in range(2, n_fsdp, 2):
        slots[j] = swap(own, "fsdp", j)
    for j in range(0, n_fsdp, 2):
        slots[j + 1] = swap(slots[j], "fsdp", 1)
    mixing = [coords]
    for j in range(1, n_grid):
        mixing.append(swap(coords, "grid", j))
    group_targets = lax.dynamic_index_in_dim(targets.reshape(n_fsdp, n_grid, sub), grid_idx, 1, False)
    group_targets = group_targets.reshape(1, tokens)
    shard = jnp.stack([shard_idx, grid_idx]).astype(jnp.int32)

    smem = pl.BlockSpec(memory_space=pltpu.SMEM)
    vmem = pl.BlockSpec(memory_space=pltpu.VMEM)
    heads = [
        pltpu.with_memory_space_constraint(w, pltpu.HBM) for w in (base_head, first_dir)
    ]
    anywhere = pl.BlockSpec(memory_space=pltpu.HBM)
    weights = pl.pallas_call(
        load_kernel,
        out_shape=tuple(pltpu.VMEM(w.shape, w.dtype) for w in heads),
        in_specs=[pl.BlockSpec(memory_space=pl.ANY)] * 3 + [anywhere] * 2,
        out_specs=(vmem,) * 2,
        scratch_shapes=[pltpu.SemaphoreType.DMA((2,))],
        compiler_params=pltpu.CompilerParams(vmem_limit_bytes=1024 * 1024),
        cost_estimate=pl.CostEstimate(flops=LOAD_FLOPS, transcendentals=0, bytes_accessed=4 * base_head.size),
        name="load_heads",
    )(shard, own, group_targets, *heads)
    sent = pl.pallas_call(
        functools.partial(head_kernel, n_fsdp, n_grid, pts),
        out_shape=jax.ShapeDtypeStruct((n_grid, n_fsdp, 2 * pts, tokens), jnp.float32),
        in_specs=[smem] * (1 + n_grid) + [vmem] * (n_fsdp + 4) + [anywhere],
        out_specs=vmem,
        scratch_shapes=[
            pltpu.VMEM((n_fsdp, sub, width), jnp.bfloat16),
            pltpu.VMEM(second_dir.shape, second_dir.dtype),
            pltpu.VMEM((2, vocab_count, tokens), jnp.float32),
            pltpu.SemaphoreType.DMA,
        ],
        compiler_params=pltpu.CompilerParams(vmem_limit_bytes=VMEM_LIMIT),
        name="head_stats",
    )(shard, *mixing, *slots, norm_gain.reshape(1, width), group_targets, *weights, pltpu.with_memory_space_constraint(second_dir, pltpu.HBM))
    got = lax.all_to_all(
        sent.reshape(n_grid * n_fsdp, 2 * pts, tokens), ("grid", "fsdp"), 0, 0
    ).reshape(n_grid, n_fsdp, 2 * pts, tokens)
    token_loss, mean_loss = pl.pallas_call(
        functools.partial(loss_kernel, sub),
        out_shape=(
            jax.ShapeDtypeStruct((pts, own_count), jnp.float32),
            jax.ShapeDtypeStruct((pts,), jnp.float32),
        ),
        in_specs=[smem, vmem],
        out_specs=(vmem, smem),
        compiler_params=pltpu.CompilerParams(vmem_limit_bytes=4 * 1024 * 1024),
        name="loss_join",
    )(shard, got)
    return (token_loss, mean_loss)


LOAD_FLOPS = 40_000_000
VMEM_LIMIT = 16 * 1024 * 1024


def solution(mesh):
    placed = (
        P("fsdp", None),
        P(),
        P("fsdp", None),
        P("fsdp", None),
        P("fsdp", None),
        P("grid", None),
        P(),
    )
    return jax.shard_map(
        body, mesh=mesh, in_specs=placed, out_specs=(P("grid", "fsdp"), P("grid")), check_vma=False
    )
```

time: 60.8 us -> 60.2 us (level)
  other arithmetic: 1.54 us -> 0.07 us
  blocking collectives: 10 us -> 11 us
  starting transfers between devices: 9.85 us -> 10.8 us
  waiting for transfers between devices: 16.5 us -> 15.6 us
    pallas_call x1, Pallas kernels: 8.19 us -> 5.81 us  [body(): pl.pallas_call(load_kernel, out_shape=tuple((pltpu.VMEM(w.shape, w.dtype)...]
    pallas_call x1, Pallas kernels: 10.5 us -> 12.8 us  [body(): pl.pallas_call(functools.partial(head_kernel, n_fsdp, n_grid, pts), out_s...]
    ppermute x10, waiting for transfers between devices: 16.5 us -> 15.6 us  [swap(): lax.ppermute(a, axis, [(i, i ^ mask) for i in range(lax.axis_size(axis))])]
    ppermute x10, starting transfers between devices: 9.85 us -> 10.8 us  [swap(): lax.ppermute(a, axis, [(i, i ^ mask) for i in range(lax.axis_size(axis))])]
    all_to_all x1, blocking collectives: 10 us -> 11 us  [body(): lax.all_to_all(sent.reshape(n_grid * n_fsdp, 2 * pts, tokens), ('grid', '...]
    reduce_sum x1 -> x0, other arithmetic: 0.83 us -> none  [mixing_of(): return jnp.sum(chosen * level_table, axis=2)]
    pallas_call x1 -> x0, other arithmetic: 0.63 us -> none  [body(): pl.pallas_call(functools.partial(loss_kernel, sub), out_shape=(jax.ShapeD...]
  transfers between devices with their start and end apart: 10 -> 10, of which waited for: 4 -> 4; matrix products, arithmetic and copies ran while one was open for 3% -> 2% of each run, Pallas kernels for 14% -> 10%
where the time goes in v1:
time: 60.2 us; the launch traced here: 59.9 us
  Pallas kernels  19.9 us (33%)
  waiting for transfers between devices  15.6 us (26%)
  blocking collectives  11 us (18%)
  starting transfers between devices  10.8 us (18%)
  local copies, waits for them, and re-layouts  1.92 us (3%)
  between operations  0.72 us (1%)
    ppermute x10, waiting for transfers between devices, swap(): lax.ppermute(a, axis, [(i, i ^ mask) for i in range(lax.axis_size(axis))])  15.6 us
    pallas_call x1, Pallas kernels, body(): pl.pallas_call(functools.partial(head_kernel, n_fsdp, n_grid, pts), out_s...  12.8 us
    all_to_all x1, blocking collectives, body(): lax.all_to_all(sent.reshape(n_grid * n_fsdp, 2 * pts, tokens), ('grid', '...  11 us
    ppermute x10, starting transfers between devices, swap(): lax.ppermute(a, axis, [(i, i ^ mask) for i in range(lax.axis_size(axis))])  10.8 us
    pallas_call x1, Pallas kernels, body(): pl.pallas_call(load_kernel, out_shape=tuple((pltpu.VMEM(w.shape, w.dtype)...  5.81 us
    pallas_call x1, Pallas kernels, body(): pl.pallas_call(functools.partial(loss_kernel, sub), out_shape=(jax.ShapeD...  1.31 us
  transfers between devices with their start and end apart: 10, of which 4 were waited for; matrix products, arithmetic and copies ran while one was open for 2% of the time, Pallas kernels for 10%

profile of v1, /device:TPU:0, one launch (start us, length us, event | category | flops | bytes accessed | tf_op | source)
XLA Modules:
  0.0 59.9 jit_solution(1295613395326018131)
XLA Ops:
  0.6 0.0 copy-start
  0.6 1.0 %copy-done = bf16[64,4096]{1,0:T(8,128)(2,1)S(1)} copy-done((bf16[64,4096]{1,0:T(8,128)(2,1)S(1)}, bf16[64,4096]{1,0:T(8,128)(2,1)}, u32[]{:S(2)}) %copy-start) | copy-done | bytes 524312
  1.7 5.1 %collective-permute-start.8 = (bf16[16,4096]{1,0:T(8,128)(2,1)S(1)}, bf16[16,4096]{1,0:T(8,128)(2,1)S(1)}, u32[]{:S(2)}, u32[]{:S(2)}) collective-permute-start(bf16[16,4096]{1,0:T(8,128)(2,1)S(1)} %constant_dynamic-slice_fusion.rows_ref.refs_4_), channel_id=1, source_target_pairs={{0,6},{1,7},{2,4},{3,5},{4,2},{5,3},{6,0},{7,1},{8,14},{9,15},{10,... | collective-permute-start | bytes 393224 | tf_op jit(solution)/shard_map/ppermute | solution.py:14
  6.8 0.0 collective-permute-start.6
  6.8 0.6 %collective-permute-start.4 = (bf16[16,4096]{1,0:T(8,128)(2,1)S(1)}, bf16[16,4096]{1,0:T(8,128)(2,1)S(1)}, u32[]{:S(2)}, u32[]{:S(2)}) collective-permute-start(bf16[16,4096]{1,0:T(8,128)(2,1)S(1)} %constant_dynamic-slice_fusion.rows_ref.refs_4_), channel_id=1, source_target_pairs={{0,2},{1,3},{2,0},{3,1},{4,6},{5,7},{6,4},{7,5},{8,10},{9,11},{10,... | collective-permute-start | bytes 393224 | tf_op jit(solution)/shard_map/ppermute | solution.py:14
  7.5 0.0 collective-permute-start.3
  7.5 3.8 %collective-permute-done.8.refs_10_ = bf16[16,4096]{1,0:T(8,128)(2,1)S(1)} collective-permute-done((bf16[16,4096]{1,0:T(8,128)(2,1)S(1)}, bf16[16,4096]{1,0:T(8,128)(2,1)S(1)}, u32[]{:S(2)}, u32[]{:S(2)}) %collective-permute-start.8) | collective-permute-done | bytes 131104 | tf_op jit(solution)/shard_map/ppermute | solution.py:14
  11.3 0.0 collective-permute-start.9
  11.3 6.6 %collective-permute-done.6.refs_8_ = bf16[16,4096]{1,0:T(8,128)(2,1)S(1)} collective-permute-done((bf16[16,4096]{1,0:T(8,128)(2,1)S(1)}, bf16[16,4096]{1,0:T(8,128)(2,1)S(1)}, u32[]{:S(2)}, u32[]{:S(2)}) %collective-permute-start.6) | collective-permute-done | bytes 131104 | tf_op jit(solution)/shard_map/ppermute | solution.py:14
  17.9 0.0 collective-permute-start.7
  17.9 0.0 collective-permute-done.4.refs_6_
  17.9 0.5 collective-permute-start.5
  18.4 1.5 %collective-permute-start.1 = (s32[2,2]{1,0:T(2,128)}, s32[2,2]{1,0:T(2,128)S(1)}, u32[]{:S(2)}, u32[]{:S(2)}) collective-permute-start(s32[2,2]{1,0:T(2,128)} %refs_0_.3), channel_id=1, source_target_pairs={{0,16},{8,24},{16,0},{24,8},{1,17},{9,25},{17,1},{25,9},{2,18},{10... | collective-permute-start | bytes 56 | tf_op jit(solution)/shard_map/ppermute | solution.py:14
  19.9 0.8 %reshape.21 = s32[8,4,16]{2,1,0:T(4,128)S(1)} reshape(s32[512]{0:T(512)} %param.13) | data formatting | bytes 4096 | tf_op jit(solution)/shard_map/reshape | solution.py:129
  20.7 0.1 reshape.22.target_ref.refs_13_
  20.8 0.1 pad_add_fusion.shard_ref
  20.9 0.0 copy-start.2
  20.9 5.8 %load_heads.1 = (bf16[1024,4096]{1,0:T(8,128)(2,1)S(1)}, bf16[1024,4096]{1,0:T(8,128)(2,1)S(1)}) custom-call(s32[2]{0:T(128)S(1)} %pad_add_fusion.shard_ref, bf16[16,4096]{1,0:T(8,128)(2,1)S(1)} %constant_dynamic-slice_fusion.rows_ref.refs_4_, s32[1,128]{1,0:T(1,128)S(1)} %reshape.22.target_ref.refs_13_, bf16[1024,4096]{1,0:T(8,128)(2,1)} %refs_0_.2, ...), custom_call_target="tpu_custom_call" | custom-call | flops 40000000 | bytes 16777216 | tf_op jit(solution)/shard_map/load_heads/pallas_call | solution.py:139
  26.7 0.0 collective-permute-done.1.refs_2_
  26.7 0.0 copy-done.2
  26.7 1.6 %collective-permute-start = (s32[2,2]{1,0:T(2,128)S(1)}, s32[2,2]{1,0:T(2,128)S(1)}, u32[]{:S(2)}, u32[]{:S(2)}) collective-permute-start(s32[2,2]{1,0:T(2,128)S(1)} %copy-done.2), channel_id=1, source_target_pairs={{0,8},{8,0},{16,24},{24,16},{1,9},{9,1},{17,25},{25,17},{2,10},{10... | collective-permute-start | bytes 56 | tf_op jit(solution)/shard_map/ppermute | solution.py:14
  28.3 2.1 %collective-permute-done.refs_1_ = s32[2,2]{1,0:T(2,128)S(1)} collective-permute-done((s32[2,2]{1,0:T(2,128)S(1)}, s32[2,2]{1,0:T(2,128)S(1)}, u32[]{:S(2)}, u32[]{:S(2)}) %collective-permute-start) | collective-permute-done | bytes 48 | tf_op jit(solution)/shard_map/ppermute | solution.py:14
  30.4 1.4 %collective-permute-start.2 = (s32[2,2]{1,0:T(2,128)S(1)}, s32[2,2]{1,0:T(2,128)S(1)}, u32[]{:S(2)}, u32[]{:S(2)}) collective-permute-start(s32[2,2]{1,0:T(2,128)S(1)} %copy-done.2), channel_id=1, source_target_pairs={{0,24},{8,16},{16,8},{24,0},{1,25},{9,17},{17,9},{25,1},{2,26},{10... | collective-permute-start | bytes 56 | tf_op jit(solution)/shard_map/ppermute | solution.py:14
  31.8 3.0 %collective-permute-done.2.refs_3_ = s32[2,2]{1,0:T(2,128)S(1)} collective-permute-done((s32[2,2]{1,0:T(2,128)S(1)}, s32[2,2]{1,0:T(2,128)S(1)}, u32[]{:S(2)}, u32[]{:S(2)}) %collective-permute-start.2) | collective-permute-done | bytes 48 | tf_op jit(solution)/shard_map/ppermute | solution.py:14
  34.8 0.0 collective-permute-done.3.refs_5_
  34.9 0.0 collective-permute-done.9.refs_11_
  34.9 0.0 collective-permute-done.7.refs_9_
  34.9 0.0 collective-permute-done.5.refs_7_
  34.9 0.0 copy-done.1
  34.9 12.8 %head_stats.1 = f32[4,8,4,128]{3,2,1,0:T(4,128)S(1)} custom-call(s32[2]{0:T(128)S(1)} %pad_add_fusion.shard_ref, s32[2,2]{1,0:T(2,128)S(1)} %copy-done.2, s32[2,2]{1,0:T(2,128)S(1)} %collective-permute-done.refs_1_, s32[2,2]{1,0:T(2,128)S(1)} %collective-permute-done.1.refs_2_, s32[2,2]{1,0:T(2,128)S(1)} %collective-permute-done.2.refs_3_, ...), custom_call_target="tpu_custom_call" | custom-call | tf_op jit(solution)/shard_map/head_stats/pallas_call | solution.py:149
  47.7 11.0 %all_to_all.5 = f32[32,4,128]{2,1,0:T(4,128)S(1)} all-to-all(f32[32,4,128]{2,1,0:T(4,128)S(1)} %bitcast.5), channel_id=1, replica_groups=mesh['grid'=4,'fsdp'=8] {'grid','fsdp'}, dimensions={0} | all-to-all | bytes 131072 | tf_op jit(solution)/shard_map/all_to_all | solution.py:163
  58.6 1.3 %loss_join.1 = (f32[2,64]{1,0:T(2,128)}, f32[2]{0:T(128)}) custom-call(s32[2]{0:T(128)S(1)} %pad_add_fusion.shard_ref, f32[4,8,4,128]{3,2,1,0:T(4,128)S(1)} %bitcast.6), custom_call_target="tpu_custom_call" | custom-call | tf_op jit(solution)/shard_map/loss_join/pallas_call | solution.py:166
  (3 shorter events, 0.0 us)
Async XLA Ops:
  0.6 1.0 %copy-start = (bf16[64,4096]{1,0:T(8,128)(2,1)S(1)}, bf16[64,4096]{1,0:T(8,128)(2,1)}, u32[]{:S(2)}) copy-start(bf16[64,4096]{1,0:T(8,128)(2,1)} %param.7) | copy-start | bytes 1572868
  1.7 9.6 %collective-permute-start.8 = (bf16[16,4096]{1,0:T(8,128)(2,1)S(1)}, bf16[16,4096]{1,0:T(8,128)(2,1)S(1)}, u32[]{:S(2)}, u32[]{:S(2)}) collective-permute-start(bf16[16,4096]{1,0:T(8,128)(2,1)S(1)} %constant_dynamic-slice_fusion.rows_ref.refs_4_), channel_id=1, source_target_pairs={{0,6},{1,7},{2,4},{3,5},{4,2},{5,3},{6,0},{7,1},{8,14},{9,15},{10,... | collective-permute-start | bytes 393224 | tf_op jit(solution)/shard_map/ppermute | solution.py:14
  6.8 11.1 %collective-permute-start.6 = (bf16[16,4096]{1,0:T(8,128)(2,1)S(1)}, bf16[16,4096]{1,0:T(8,128)(2,1)S(1)}, u32[]{:S(2)}, u32[]{:S(2)}) collective-permute-start(bf16[16,4096]{1,0:T(8,128)(2,1)S(1)} %constant_dynamic-slice_fusion.rows_ref.refs_4_), channel_id=1, source_target_pairs={{0,4},{1,5},{2,6},{3,7},{4,0},{5,1},{6,2},{7,3},{8,12},{9,13},{10,... | collective-permute-start | bytes 393224 | tf_op jit(solution)/shard_map/ppermute | solution.py:14
  6.8 11.1 %collective-permute-start.4 = (bf16[16,4096]{1,0:T(8,128)(2,1)S(1)}, bf16[16,4096]{1,0:T(8,128)(2,1)S(1)}, u32[]{:S(2)}, u32[]{:S(2)}) collective-permute-start(bf16[16,4096]{1,0:T(8,128)(2,1)S(1)} %constant_dynamic-slice_fusion.rows_ref.refs_4_), channel_id=1, source_target_pairs={{0,2},{1,3},{2,0},{3,1},{4,6},{5,7},{6,4},{7,5},{8,10},{9,11},{10,... | collective-permute-start | bytes 393224 | tf_op jit(solution)/shard_map/ppermute | solution.py:14
  7.5 27.4 %collective-permute-start.3 = (bf16[16,4096]{1,0:T(8,128)(2,1)S(1)}, bf16[16,4096]{1,0:T(8,128)(2,1)S(1)}, u32[]{:S(2)}, u32[]{:S(2)}) collective-permute-start(bf16[16,4096]{1,0:T(8,128)(2,1)S(1)} %constant_dynamic-slice_fusion.rows_ref.refs_4_), channel_id=1, source_target_pairs={{0,1},{1,0},{2,3},{3,2},{4,5},{5,4},{6,7},{7,6},{8,9},{9,8},{10,11... | collective-permute-start | bytes 393224 | tf_op jit(solution)/shard_map/ppermute | solution.py:14
  11.3 23.6 %collective-permute-start.9 = (bf16[16,4096]{1,0:T(8,128)(2,1)S(1)}, bf16[16,4096]{1,0:T(8,128)(2,1)S(1)}, u32[]{:S(2)}, u32[]{:S(2)}) collective-permute-start(bf16[16,4096]{1,0:T(8,128)(2,1)S(1)} %collective-permute-done.8.refs_10_), channel_id=1, source_target_pairs={{0,1},{1,0},{2,3},{3,2},{4,5},{5,4},{6,7},{7,6},{8,9},{9,8},{10,11... | collective-permute-start | bytes 393224 | tf_op jit(solution)/shard_map/ppermute | solution.py:14
  17.9 16.9 %collective-permute-start.7 = (bf16[16,4096]{1,0:T(8,128)(2,1)S(1)}, bf16[16,4096]{1,0:T(8,128)(2,1)S(1)}, u32[]{:S(2)}, u32[]{:S(2)}) collective-permute-start(bf16[16,4096]{1,0:T(8,128)(2,1)S(1)} %collective-permute-done.6.refs_8_), channel_id=1, source_target_pairs={{0,1},{1,0},{2,3},{3,2},{4,5},{5,4},{6,7},{7,6},{8,9},{9,8},{10,11... | collective-permute-start | bytes 393224 | tf_op jit(solution)/shard_map/ppermute | solution.py:14
  17.9 16.9 %collective-permute-start.5 = (bf16[16,4096]{1,0:T(8,128)(2,1)S(1)}, bf16[16,4096]{1,0:T(8,128)(2,1)S(1)}, u32[]{:S(2)}, u32[]{:S(2)}) collective-permute-start(bf16[16,4096]{1,0:T(8,128)(2,1)S(1)} %collective-permute-done.4.refs_6_), channel_id=1, source_target_pairs={{0,1},{1,0},{2,3},{3,2},{4,5},{5,4},{6,7},{7,6},{8,9},{9,8},{10,11... | collective-permute-start | bytes 393224 | tf_op jit(solution)/shard_map/ppermute | solution.py:14
  18.4 8.3 %collective-permute-start.1 = (s32[2,2]{1,0:T(2,128)}, s32[2,2]{1,0:T(2,128)S(1)}, u32[]{:S(2)}, u32[]{:S(2)}) collective-permute-start(s32[2,2]{1,0:T(2,128)} %refs_0_.3), channel_id=1, source_target_pairs={{0,16},{8,24},{16,0},{24,8},{1,17},{9,25},{17,1},{25,9},{2,18},{10... | collective-permute-start | bytes 56 | tf_op jit(solution)/shard_map/ppermute | solution.py:14
  20.9 5.8 %copy-start.2 = (s32[2,2]{1,0:T(2,128)S(1)}, s32[2,2]{1,0:T(2,128)}, u32[]{:S(2)}) copy-start(s32[2,2]{1,0:T(2,128)} %refs_0_.3) | copy-start | bytes 52
  20.9 14.0 %copy-start.1 = (f32[4096]{0:T(1024)S(1)}, f32[4096]{0:T(1024)}, u32[]{:S(2)}) copy-start(f32[4096]{0:T(1024)} %param.8) | copy-start | bytes 49156
  26.7 3.6 %collective-permute-start = (s32[2,2]{1,0:T(2,128)S(1)}, s32[2,2]{1,0:T(2,128)S(1)}, u32[]{:S(2)}, u32[]{:S(2)}) collective-permute-start(s32[2,2]{1,0:T(2,128)S(1)} %copy-done.2), channel_id=1, source_target_pairs={{0,8},{8,0},{16,24},{24,16},{1,9},{9,1},{17,25},{25,17},{2,10},{10... | collective-permute-start | bytes 56 | tf_op jit(solution)/shard_map/ppermute | solution.py:14
  30.4 4.5 %collective-permute-start.2 = (s32[2,2]{1,0:T(2,128)S(1)}, s32[2,2]{1,0:T(2,128)S(1)}, u32[]{:S(2)}, u32[]{:S(2)}) collective-permute-start(s32[2,2]{1,0:T(2,128)S(1)} %copy-done.2), channel_id=1, source_target_pairs={{0,24},{8,16},{16,8},{24,0},{1,25},{9,17},{17,9},{25,1},{2,26},{10... | collective-permute-start | bytes 56 | tf_op jit(solution)/shard_map/ppermute | solution.py:14

commit v2 on v1

--- a/solution.py
+++ b/solution.py
@@ -17,10 +17,8 @@
 def head_kernel(n_fsdp, n_grid, pts, shard_ref, *refs):
     coords_refs, refs = refs[:n_grid], refs[n_grid:]
     chunks, refs = refs[:n_fsdp], refs[n_fsdp:]
-    gain_ref, target_ref, base_ref, first_ref, second_hbm, out_ref = refs[:6]
-    rows_ref, second_ref, dots_ref, arrived = refs[6:]
-    fetch = pltpu.make_async_copy(second_hbm, second_ref, arrived)
-    fetch.start()
+    gain_ref, target_ref, base_ref, first_ref, second_ref, out_ref = refs[:6]
+    rows_ref, dots_ref = refs[6:]
     shard_idx, grid_idx = shard_ref[0], shard_ref[1]
     for j in range(n_fsdp):
         widened = chunks[j][...].astype(jnp.float32)
@@ -38,7 +36,6 @@
 
     dots_ref[0] = dot_of(base_ref[...])
     dots_ref[1] = dot_of(first_ref[...])
-    fetch.wait()
     points = []
     for j in range(n_grid):
         for p in range(pts):
@@ -80,11 +77,21 @@
             out_ref[grid_idx ^ j, f] = packed
 
 
+def copies_of(pairs, arrived):
+    copies = []
+    for source, target in pairs:
+        count = source.shape[0] // PIECES
+        for piece in range(PIECES):
+            span = pl.ds(piece * count, count)
+            copies.append(
+                pltpu.make_async_copy(source.at[span], target.at[span], arrived.at[len(copies)])
+            )
+    return copies
+
+
 def load_kernel(shard_ref, rows_ref, target_ref, *refs):
     count = (len(refs) - 1) // 2
-    copies = [
-        pltpu.make_async_copy(refs[k], refs[count + k], refs[-1].at[k]) for k in range(count)
-    ]
+    copies = copies_of(list(zip(refs[:count], refs[count : 2 * count])), refs[-1])
     for copy in copies:
         copy.start()
     for copy in copies:
@@ -133,15 +140,15 @@
     smem = pl.BlockSpec(memory_space=pltpu.SMEM)
     vmem = pl.BlockSpec(memory_space=pltpu.VMEM)
     heads = [
-        pltpu.with_memory_space_constraint(w, pltpu.HBM) for w in (base_head, first_dir)
+        pltpu.with_memory_space_constraint(w, pltpu.HBM) for w in (base_head, first_dir, second_dir)
     ]
     anywhere = pl.BlockSpec(memory_space=pltpu.HBM)
     weights = pl.pallas_call(
         load_kernel,
         out_shape=tuple(pltpu.VMEM(w.shape, w.dtype) for w in heads),
-        in_specs=[pl.BlockSpec(memory_space=pl.ANY)] * 3 + [anywhere] * 2,
-        out_specs=(vmem,) * 2,
-        scratch_shapes=[pltpu.SemaphoreType.DMA((2,))],
+        in_specs=[pl.BlockSpec(memory_space=pl.ANY)] * 3 + [anywhere] * 3,
+        out_specs=(vmem,) * 3,
+        scratch_shapes=[pltpu.SemaphoreType.DMA((3 * PIECES,))],
         compiler_params=pltpu.CompilerParams(vmem_limit_bytes=1024 * 1024),
         cost_estimate=pl.CostEstimate(flops=LOAD_FLOPS, transcendentals=0, bytes_accessed=4 * base_head.size),
         name="load_heads",
@@ -149,17 +156,15 @@
     sent = pl.pallas_call(
         functools.partial(head_kernel, n_fsdp, n_grid, pts),
         out_shape=jax.ShapeDtypeStruct((n_grid, n_fsdp, 2 * pts, tokens), jnp.float32),
-        in_specs=[smem] * (1 + n_grid) + [vmem] * (n_fsdp + 4) + [anywhere],
+        in_specs=[smem] * (1 + n_grid) + [vmem] * (n_fsdp + 5),
         out_specs=vmem,
         scratch_shapes=[
             pltpu.VMEM((n_fsdp, sub, width), jnp.bfloat16),
-            pltpu.VMEM(second_dir.shape, second_dir.dtype),
             pltpu.VMEM((2, vocab_count, tokens), jnp.float32),
-            pltpu.SemaphoreType.DMA,
         ],
         compiler_params=pltpu.CompilerParams(vmem_limit_bytes=VMEM_LIMIT),
         name="head_stats",
-    )(shard, *mixing, *slots, norm_gain.reshape(1, width), group_targets, *weights, pltpu.with_memory_space_constraint(second_dir, pltpu.HBM))
+    )(shard, *mixing, *slots, norm_gain.reshape(1, width), group_targets, *weights)
     got = lax.all_to_all(
         sent.reshape(n_grid * n_fsdp, 2 * pts, tokens), ("grid", "fsdp"), 0, 0
     ).reshape(n_grid, n_fsdp, 2 * pts, tokens)
@@ -178,6 +183,7 @@
 
 
 LOAD_FLOPS = 40_000_000
+PIECES = 4
 VMEM_LIMIT = 16 * 1024 * 1024
 
 

time: 60.2 us -> 59.1 us (0.982)
  Pallas kernels: 19.9 us -> 18.9 us
    pallas_call x1, Pallas kernels: 12.8 us -> 9.22 us  [body(): pl.pallas_call(functools.partial(head_kernel, n_fsdp, n_grid, pts), out_s...]
    pallas_call x1, Pallas kernels: 5.81 us -> 8.36 us  [body(): pl.pallas_call(load_kernel, out_shape=tuple((pltpu.VMEM(w.shape, w.dtype)...]
  transfers between devices with their start and end apart: 10 -> 10, of which waited for: 4 -> 4; matrix products, arithmetic and copies ran while one was open for 2% -> 2% of each run, Pallas kernels for 10% -> 14%
where the time goes in v2:
time: 59.1 us; the launch traced here: 58.9 us
  Pallas kernels  18.9 us (32%)
  waiting for transfers between devices  15.6 us (26%)
  blocking collectives  11 us (19%)
  starting transfers between devices  10.8 us (18%)
  local copies, waits for them, and re-layouts  1.92 us (3%)
  between operations  0.71 us (1%)
    ppermute x10, waiting for transfers between devices, swap(): lax.ppermute(a, axis, [(i, i ^ mask) for i in range(lax.axis_size(axis))])  15.6 us
    all_to_all x1, blocking collectives, body(): lax.all_to_all(sent.reshape(n_grid * n_fsdp, 2 * pts, tokens), ('grid', '...  11 us
    ppermute x10, starting transfers between devices, swap(): lax.ppermute(a, axis, [(i, i ^ mask) for i in range(lax.axis_size(axis))])  10.8 us
    pallas_call x1, Pallas kernels, body(): pl.pallas_call(functools.partial(head_kernel, n_fsdp, n_grid, pts), out_s...  9.22 us
    pallas_call x1, Pallas kernels, body(): pl.pallas_call(load_kernel, out_shape=tuple((pltpu.VMEM(w.shape, w.dtype)...  8.36 us
    pallas_call x1, Pallas kernels, body(): pl.pallas_call(functools.partial(loss_kernel, sub), out_shape=(jax.ShapeD...  1.31 us
  transfers between devices with their start and end apart: 10, of which 4 were waited for; matrix products, arithmetic and copies ran while one was open for 2% of the time, Pallas kernels for 14%

profile of v2, /device:TPU:0, one launch (start us, length us, event | category | flops | bytes accessed | tf_op | source)
XLA Modules:
  0.0 58.9 jit_solution(9053733103229343831)
XLA Ops:
  0.6 0.0 copy-start
  0.6 1.0 %copy-done = bf16[64,4096]{1,0:T(8,128)(2,1)S(1)} copy-done((bf16[64,4096]{1,0:T(8,128)(2,1)S(1)}, bf16[64,4096]{1,0:T(8,128)(2,1)}, u32[]{:S(2)}) %copy-start) | copy-done | bytes 524312
  1.7 5.1 %collective-permute-start.8 = (bf16[16,4096]{1,0:T(8,128)(2,1)S(1)}, bf16[16,4096]{1,0:T(8,128)(2,1)S(1)}, u32[]{:S(2)}, u32[]{:S(2)}) collective-permute-start(bf16[16,4096]{1,0:T(8,128)(2,1)S(1)} %constant_dynamic-slice_fusion.rows_ref.refs_4_), channel_id=1, source_target_pairs={{0,6},{1,7},{2,4},{3,5},{4,2},{5,3},{6,0},{7,1},{8,14},{9,15},{10,... | collective-permute-start | bytes 393224 | tf_op jit(solution)/shard_map/ppermute | solution.py:14
  6.8 0.0 collective-permute-start.6
  6.8 0.6 %collective-permute-start.4 = (bf16[16,4096]{1,0:T(8,128)(2,1)S(1)}, bf16[16,4096]{1,0:T(8,128)(2,1)S(1)}, u32[]{:S(2)}, u32[]{:S(2)}) collective-permute-start(bf16[16,4096]{1,0:T(8,128)(2,1)S(1)} %constant_dynamic-slice_fusion.rows_ref.refs_4_), channel_id=1, source_target_pairs={{0,2},{1,3},{2,0},{3,1},{4,6},{5,7},{6,4},{7,5},{8,10},{9,11},{10,... | collective-permute-start | bytes 393224 | tf_op jit(solution)/shard_map/ppermute | solution.py:14
  7.5 0.0 collective-permute-start.3
  7.5 3.8 %collective-permute-done.8.refs_10_ = bf16[16,4096]{1,0:T(8,128)(2,1)S(1)} collective-permute-done((bf16[16,4096]{1,0:T(8,128)(2,1)S(1)}, bf16[16,4096]{1,0:T(8,128)(2,1)S(1)}, u32[]{:S(2)}, u32[]{:S(2)}) %collective-permute-start.8) | collective-permute-done | bytes 131104 | tf_op jit(solution)/shard_map/ppermute | solution.py:14
  11.3 0.0 collective-permute-start.9
  11.3 6.6 %collective-permute-done.6.refs_8_ = bf16[16,4096]{1,0:T(8,128)(2,1)S(1)} collective-permute-done((bf16[16,4096]{1,0:T(8,128)(2,1)S(1)}, bf16[16,4096]{1,0:T(8,128)(2,1)S(1)}, u32[]{:S(2)}, u32[]{:S(2)}) %collective-permute-start.6) | collective-permute-done | bytes 131104 | tf_op jit(solution)/shard_map/ppermute | solution.py:14
  17.9 0.0 collective-permute-start.7
  17.9 0.0 collective-permute-done.4.refs_6_
  17.9 0.5 collective-permute-start.5
  18.4 1.5 %collective-permute-start.1 = (s32[2,2]{1,0:T(2,128)}, s32[2,2]{1,0:T(2,128)S(1)}, u32[]{:S(2)}, u32[]{:S(2)}) collective-permute-start(s32[2,2]{1,0:T(2,128)} %refs_0_.3), channel_id=1, source_target_pairs={{0,16},{8,24},{16,0},{24,8},{1,17},{9,25},{17,1},{25,9},{2,18},{10... | collective-permute-start | bytes 56 | tf_op jit(solution)/shard_map/ppermute | solution.py:14
  19.9 0.8 %reshape.21 = s32[8,4,16]{2,1,0:T(4,128)S(1)} reshape(s32[512]{0:T(512)} %param.13) | data formatting | bytes 4096 | tf_op jit(solution)/shard_map/reshape | solution.py:136
  20.7 0.1 reshape.22.target_ref.refs_13_
  20.8 0.1 pad_add_fusion.shard_ref
  20.9 0.0 copy-start.2
  20.9 8.4 %load_heads.1 = (bf16[1024,4096]{1,0:T(8,128)(2,1)S(1)}, bf16[1024,4096]{1,0:T(8,128)(2,1)S(1)}, bf16[1024,4096]{1,0:T(8,128)(2,1)S(1)}) custom-call(s32[2]{0:T(128)S(1)} %pad_add_fusion.shard_ref, bf16[16,4096]{1,0:T(8,128)(2,1)S(1)} %constant_dynamic-slice_fusion.rows_ref.refs_4_, s32[1,128]{1,0:T(1,128)S(1)} %reshape.22.target_ref.refs_13_, ...), custom_call_target="tpu_custom_call" | custom-call | flops 40000000 | bytes 16777216 | tf_op jit(solution)/shard_map/load_heads/pallas_call | solution.py:146
  29.3 0.0 collective-permute-done.1.refs_2_
  29.3 0.0 copy-done.2
  29.3 1.6 %collective-permute-start = (s32[2,2]{1,0:T(2,128)S(1)}, s32[2,2]{1,0:T(2,128)S(1)}, u32[]{:S(2)}, u32[]{:S(2)}) collective-permute-start(s32[2,2]{1,0:T(2,128)S(1)} %copy-done.2), channel_id=1, source_target_pairs={{0,8},{8,0},{16,24},{24,16},{1,9},{9,1},{17,25},{25,17},{2,10},{10... | collective-permute-start | bytes 56 | tf_op jit(solution)/shard_map/ppermute | solution.py:14
  30.8 2.1 %collective-permute-done.refs_1_ = s32[2,2]{1,0:T(2,128)S(1)} collective-permute-done((s32[2,2]{1,0:T(2,128)S(1)}, s32[2,2]{1,0:T(2,128)S(1)}, u32[]{:S(2)}, u32[]{:S(2)}) %collective-permute-start) | collective-permute-done | bytes 48 | tf_op jit(solution)/shard_map/ppermute | solution.py:14
  32.9 1.4 %collective-permute-start.2 = (s32[2,2]{1,0:T(2,128)S(1)}, s32[2,2]{1,0:T(2,128)S(1)}, u32[]{:S(2)}, u32[]{:S(2)}) collective-permute-start(s32[2,2]{1,0:T(2,128)S(1)} %copy-done.2), channel_id=1, source_target_pairs={{0,24},{8,16},{16,8},{24,0},{1,25},{9,17},{17,9},{25,1},{2,26},{10... | collective-permute-start | bytes 56 | tf_op jit(solution)/shard_map/ppermute | solution.py:14
  34.4 3.0 %collective-permute-done.2.refs_3_ = s32[2,2]{1,0:T(2,128)S(1)} collective-permute-done((s32[2,2]{1,0:T(2,128)S(1)}, s32[2,2]{1,0:T(2,128)S(1)}, u32[]{:S(2)}, u32[]{:S(2)}) %collective-permute-start.2) | collective-permute-done | bytes 48 | tf_op jit(solution)/shard_map/ppermute | solution.py:14
  37.4 0.0 collective-permute-done.3.refs_5_
  37.4 0.0 collective-permute-done.9.refs_11_
  37.4 0.0 collective-permute-done.7.refs_9_
  37.4 0.0 collective-permute-done.5.refs_7_
  37.4 0.0 copy-done.1
  37.4 9.2 %head_stats.1 = f32[4,8,4,128]{3,2,1,0:T(4,128)S(1)} custom-call(s32[2]{0:T(128)S(1)} %pad_add_fusion.shard_ref, s32[2,2]{1,0:T(2,128)S(1)} %copy-done.2, s32[2,2]{1,0:T(2,128)S(1)} %collective-permute-done.refs_1_, s32[2,2]{1,0:T(2,128)S(1)} %collective-permute-done.1.refs_2_, s32[2,2]{1,0:T(2,128)S(1)} %collective-permute-done.2.refs_3_, ...), custom_call_target="tpu_custom_call" | custom-call | tf_op jit(solution)/shard_map/head_stats/pallas_call | solution.py:156
  46.7 11.0 %all_to_all.5 = f32[32,4,128]{2,1,0:T(4,128)S(1)} all-to-all(f32[32,4,128]{2,1,0:T(4,128)S(1)} %bitcast.5), channel_id=1, replica_groups=mesh['grid'=4,'fsdp'=8] {'grid','fsdp'}, dimensions={0} | all-to-all | bytes 131072 | tf_op jit(solution)/shard_map/all_to_all | solution.py:168
  57.6 1.3 %loss_join.1 = (f32[2,64]{1,0:T(2,128)}, f32[2]{0:T(128)}) custom-call(s32[2]{0:T(128)S(1)} %pad_add_fusion.shard_ref, f32[4,8,4,128]{3,2,1,0:T(4,128)S(1)} %bitcast.6), custom_call_target="tpu_custom_call" | custom-call | tf_op jit(solution)/shard_map/loss_join/pallas_call | solution.py:171
  (3 shorter events, 0.0 us)
Async XLA Ops:
  0.6 1.0 %copy-start = (bf16[64,4096]{1,0:T(8,128)(2,1)S(1)}, bf16[64,4096]{1,0:T(8,128)(2,1)}, u32[]{:S(2)}) copy-start(bf16[64,4096]{1,0:T(8,128)(2,1)} %param.7) | copy-start | bytes 1572868
  1.7 9.6 %collective-permute-start.8 = (bf16[16,4096]{1,0:T(8,128)(2,1)S(1)}, bf16[16,4096]{1,0:T(8,128)(2,1)S(1)}, u32[]{:S(2)}, u32[]{:S(2)}) collective-permute-start(bf16[16,4096]{1,0:T(8,128)(2,1)S(1)} %constant_dynamic-slice_fusion.rows_ref.refs_4_), channel_id=1, source_target_pairs={{0,6},{1,7},{2,4},{3,5},{4,2},{5,3},{6,0},{7,1},{8,14},{9,15},{10,... | collective-permute-start | bytes 393224 | tf_op jit(solution)/shard_map/ppermute | solution.py:14
  6.8 11.1 %collective-permute-start.6 = (bf16[16,4096]{1,0:T(8,128)(2,1)S(1)}, bf16[16,4096]{1,0:T(8,128)(2,1)S(1)}, u32[]{:S(2)}, u32[]{:S(2)}) collective-permute-start(bf16[16,4096]{1,0:T(8,128)(2,1)S(1)} %constant_dynamic-slice_fusion.rows_ref.refs_4_), channel_id=1, source_target_pairs={{0,4},{1,5},{2,6},{3,7},{4,0},{5,1},{6,2},{7,3},{8,12},{9,13},{10,... | collective-permute-start | bytes 393224 | tf_op jit(solution)/shard_map/ppermute | solution.py:14
  6.8 11.1 %collective-permute-start.4 = (bf16[16,4096]{1,0:T(8,128)(2,1)S(1)}, bf16[16,4096]{1,0:T(8,128)(2,1)S(1)}, u32[]{:S(2)}, u32[]{:S(2)}) collective-permute-start(bf16[16,4096]{1,0:T(8,128)(2,1)S(1)} %constant_dynamic-slice_fusion.rows_ref.refs_4_), channel_id=1, source_target_pairs={{0,2},{1,3},{2,0},{3,1},{4,6},{5,7},{6,4},{7,5},{8,10},{9,11},{10,... | collective-permute-start | bytes 393224 | tf_op jit(solution)/shard_map/ppermute | solution.py:14
  7.5 29.9 %collective-permute-start.3 = (bf16[16,4096]{1,0:T(8,128)(2,1)S(1)}, bf16[16,4096]{1,0:T(8,128)(2,1)S(1)}, u32[]{:S(2)}, u32[]{:S(2)}) collective-permute-start(bf16[16,4096]{1,0:T(8,128)(2,1)S(1)} %constant_dynamic-slice_fusion.rows_ref.refs_4_), channel_id=1, source_target_pairs={{0,1},{1,0},{2,3},{3,2},{4,5},{5,4},{6,7},{7,6},{8,9},{9,8},{10,11... | collective-permute-start | bytes 393224 | tf_op jit(solution)/shard_map/ppermute | solution.py:14
  11.3 26.1 %collective-permute-start.9 = (bf16[16,4096]{1,0:T(8,128)(2,1)S(1)}, bf16[16,4096]{1,0:T(8,128)(2,1)S(1)}, u32[]{:S(2)}, u32[]{:S(2)}) collective-permute-start(bf16[16,4096]{1,0:T(8,128)(2,1)S(1)} %collective-permute-done.8.refs_10_), channel_id=1, source_target_pairs={{0,1},{1,0},{2,3},{3,2},{4,5},{5,4},{6,7},{7,6},{8,9},{9,8},{10,11... | collective-permute-start | bytes 393224 | tf_op jit(solution)/shard_map/ppermute | solution.py:14
  17.9 19.5 %collective-permute-start.7 = (bf16[16,4096]{1,0:T(8,128)(2,1)S(1)}, bf16[16,4096]{1,0:T(8,128)(2,1)S(1)}, u32[]{:S(2)}, u32[]{:S(2)}) collective-permute-start(bf16[16,4096]{1,0:T(8,128)(2,1)S(1)} %collective-permute-done.6.refs_8_), channel_id=1, source_target_pairs={{0,1},{1,0},{2,3},{3,2},{4,5},{5,4},{6,7},{7,6},{8,9},{9,8},{10,11... | collective-permute-start | bytes 393224 | tf_op jit(solution)/shard_map/ppermute | solution.py:14
  17.9 19.5 %collective-permute-start.5 = (bf16[16,4096]{1,0:T(8,128)(2,1)S(1)}, bf16[16,4096]{1,0:T(8,128)(2,1)S(1)}, u32[]{:S(2)}, u32[]{:S(2)}) collective-permute-start(bf16[16,4096]{1,0:T(8,128)(2,1)S(1)} %collective-permute-done.4.refs_6_), channel_id=1, source_target_pairs={{0,1},{1,0},{2,3},{3,2},{4,5},{5,4},{6,7},{7,6},{8,9},{9,8},{10,11... | collective-permute-start | bytes 393224 | tf_op jit(solution)/shard_map/ppermute | solution.py:14
  18.4 10.8 %collective-permute-start.1 = (s32[2,2]{1,0:T(2,128)}, s32[2,2]{1,0:T(2,128)S(1)}, u32[]{:S(2)}, u32[]{:S(2)}) collective-permute-start(s32[2,2]{1,0:T(2,128)} %refs_0_.3), channel_id=1, source_target_pairs={{0,16},{8,24},{16,0},{24,8},{1,17},{9,25},{17,1},{25,9},{2,18},{10... | collective-permute-start | bytes 56 | tf_op jit(solution)/shard_map/ppermute | solution.py:14
  20.9 8.4 %copy-start.2 = (s32[2,2]{1,0:T(2,128)S(1)}, s32[2,2]{1,0:T(2,128)}, u32[]{:S(2)}) copy-start(s32[2,2]{1,0:T(2,128)} %refs_0_.3) | copy-start | bytes 52
  20.9 16.5 %copy-start.1 = (f32[4096]{0:T(1024)S(1)}, f32[4096]{0:T(1024)}, u32[]{:S(2)}) copy-start(f32[4096]{0:T(1024)} %param.8) | copy-start | bytes 49156
  29.3 3.6 %collective-permute-start = (s32[2,2]{1,0:T(2,128)S(1)}, s32[2,2]{1,0:T(2,128)S(1)}, u32[]{:S(2)}, u32[]{:S(2)}) collective-permute-start(s32[2,2]{1,0:T(2,128)S(1)} %copy-done.2), channel_id=1, source_target_pairs={{0,8},{8,0},{16,24},{24,16},{1,9},{9,1},{17,25},{25,17},{2,10},{10... | collective-permute-start | bytes 56 | tf_op jit(solution)/shard_map/ppermute | solution.py:14
  32.9 4.5 %collective-permute-start.2 = (s32[2,2]{1,0:T(2,128)S(1)}, s32[2,2]{1,0:T(2,128)S(1)}, u32[]{:S(2)}, u32[]{:S(2)}) collective-permute-start(s32[2,2]{1,0:T(2,128)S(1)} %copy-done.2), channel_id=1, source_target_pairs={{0,24},{8,16},{16,8},{24,0},{1,25},{9,17},{17,9},{25,1},{2,26},{10... | collective-permute-start | bytes 56 | tf_op jit(solution)/shard_map/ppermute | solution.py:14
